TPU v7x, 16 devices: a 4x2x1 block of a 4x4x8 slice. The times are simulated.
16 devices in a mesh: dp: 2 (over y, z), sp: 8 (over x, core).
Axes of the slice: x: 4, y: 2, z: 1, core: 2. Of those that a mesh axis runs over, the one named last changes fastest.
The devices are a block of a 4x4x8 slice.
Arguments:
- resid_x: bfloat16 [32, 1024, 2048], P('dp', 'sp'), parts along dimension 0
- positions: int32 [32, 1024], P('dp', 'sp'), parts along dimension 0
- w_query: bfloat16 [2048, 2048], replicated
- w_key: bfloat16 [2048, 2048], replicated
- w_value: bfloat16 [2048, 2048], replicated
- w_out: bfloat16 [2048, 2048], replicated
- gain_q: bfloat16 [2048], replicated
- gain_k: bfloat16 [2048], replicated
- gain_out: bfloat16 [2048], replicated
Outputs:
- output: bfloat16 [32, 1024, 2048], P('dp', 'sp'), parts along dimension 0
There are 2 independent parts. A program takes and returns all parts, laid end to end along the dimension named above; an argument that names none is the same for every part.
All inputs are finite; a program needn't handle non-finite values.
Results may differ from a plain program's by a relative error of at most 0.0178911.
Values are sent between devices in bfloat16 or wider.
A program may use at most 768 MiB of HBM per device.

v0:
```python
import jax
import jax.numpy as jnp
from jax import lax
from jax.sharding import PartitionSpec as P

HEAD_DIM = 128
QUERY_BLOCKS = 8
ROPE_THETA = 500000.0
NORM_EPS = 1e-6
SCALE = HEAD_DIM ** -0.5


def rope_tables(pos_ids):
    inv_freq = 1.0 / (ROPE_THETA ** (jnp.arange(0, HEAD_DIM, 2, dtype=jnp.float32) / HEAD_DIM))
    angles = pos_ids.astype(jnp.float32)[..., None] * inv_freq
    return jnp.cos(angles), jnp.sin(angles)


def apply_rope(heads_f32, cos_t, sin_t):
    half = HEAD_DIM // 2
    cos_b = cos_t[:, :, None, :]
    sin_b = sin_t[:, :, None, :]
    first = heads_f32[..., :half]
    second = heads_f32[..., half:]
    return jnp.concatenate([first * cos_b - second * sin_b, second * cos_b + first * sin_b], axis=-1)


def rms_scale(vals_f32, gain):
    mean_sq = jnp.mean(vals_f32 * vals_f32, axis=-1, keepdims=True)
    return vals_f32 * lax.rsqrt(mean_sq + NORM_EPS) * gain.astype(jnp.float32)


def project(x_tok, weight):
    return jnp.einsum('bsd,de->bse', x_tok, weight, preferred_element_type=jnp.float32).astype(jnp.bfloat16)


def norm_rope(x_tok, weight, gain, cos_t, sin_t):
    proj = project(x_tok, weight).astype(jnp.float32)
    batch, seq_len, model_width = proj.shape
    normed = rms_scale(proj, gain).reshape(batch, seq_len, model_width // HEAD_DIM, HEAD_DIM)
    return apply_rope(normed, cos_t, sin_t).astype(jnp.bfloat16)


def causal_attention(q_heads, k_heads, v_heads):
    seq_len = q_heads.shape[1]
    block = seq_len // QUERY_BLOCKS
    outs = []
    for blk_idx in range(QUERY_BLOCKS):
        key_end = (blk_idx + 1) * block
        q_blk = q_heads[:, blk_idx * block:key_end]
        scores = jnp.einsum('bqhd,bkhd->bhqk', q_blk, k_heads[:, :key_end], preferred_element_type=jnp.float32) * SCALE
        q_idx = blk_idx * block + jnp.arange(block)
        scores = jnp.where(jnp.arange(key_end)[None, :] <= q_idx[:, None], scores, -1e30)
        probs = jax.nn.softmax(scores, axis=-1).astype(jnp.bfloat16)
        outs.append(jnp.einsum('bhqk,bkhd->bqhd', probs, v_heads[:, :key_end], preferred_element_type=jnp.float32).astype(jnp.bfloat16))
    return jnp.concatenate(outs, axis=1)


def solution(mesh):
    def local_block(x_loc, pos_loc, w_query, w_key, w_value, w_out, gain_q, gain_k, gain_out):
        batch, seq_loc, model_width = x_loc.shape
        cos_t, sin_t = rope_tables(pos_loc)
        q_loc = norm_rope(x_loc, w_query, gain_q, cos_t, sin_t)
        k_loc = norm_rope(x_loc, w_key, gain_k, cos_t, sin_t)
        v_loc = project(x_loc, w_value).reshape(batch, seq_loc, model_width // HEAD_DIM, HEAD_DIM)
        q_heads = lax.all_to_all(q_loc, 'sp', 2, 1, tiled=True)
        k_heads = lax.all_to_all(k_loc, 'sp', 2, 1, tiled=True)
        v_heads = lax.all_to_all(v_loc, 'sp', 2, 1, tiled=True)
        o_heads = causal_attention(q_heads, k_heads, v_heads)
        o_loc = lax.all_to_all(o_heads, 'sp', 1, 2, tiled=True).reshape(batch, seq_loc, model_width)
        attn_out = project(o_loc, w_out).astype(jnp.float32)
        return (x_loc.astype(jnp.float32) + rms_scale(attn_out, gain_out)).astype(jnp.bfloat16)

    tok_spec = P('dp', 'sp', None)
    return jax.shard_map(local_block, mesh=mesh, in_specs=(tok_spec, P('dp', 'sp'), P(), P(), P(), P(), P(), P(), P()), out_specs=tok_spec, check_vma=False)
```

profile of v0, /device:TPU:113, one launch (start us, length us, event | category | flops | bytes accessed | tf_op | source)
XLA Modules:
  0.0 816.9 jit_solution(9639015662523360941)
XLA Ops:
  0.6 23.6 %fusion.8 = (f32[16,128]{1,0:T(8,128)S(1)}, bf16[16,128,2048]{2,1,0:T(8,128)(2,1)}) fusion(bf16[16,128,2048]{2,1,0:T(8,128)(2,1)} %param.9, bf16[2048,2048]{1,0:T(8,128)(2,1)} %param.11), kind=kOutput, calls=%fused_computation.14 | convolution fusion | flops 17196644352 | bytes 25174016 | tf_op jit(solution)/shard_map/bsd,de->bse/dot_general | solution.py:34
  24.2 11.0 %fusion.9 = f32[16,128,2048]{2,1,0:T(8,128)} fusion(bf16[16,128,2048]{2,1,0:T(8,128)(2,1)} %get-tuple-element.18, f32[2048]{0:T(1024)S(1)} %convert_element_type.117, f32[16,128]{1,0:T(8,128)S(1)} %add_rsqrt_fusion.2), kind=kLoop, calls=%fused_computation.15 | loop fusion | flops 12582912 | bytes 25182208 | tf_op jit(solution)/shard_map/mul | solution.py:30
  35.2 14.3 %copy.32 = f32[256,8,16,128]{3,2,1,0:T(8,128)} copy(f32[256,8,16,128]{3,1,2,0:T(8,128)} %bitcast.107) | data formatting | bytes 33554432
  49.5 22.2 %fusion.10 = (f32[16,128]{1,0:T(8,128)S(1)}, bf16[16,128,2048]{2,1,0:T(8,128)(2,1)}) fusion(bf16[16,128,2048]{2,1,0:T(8,128)(2,1)S(1)} %bitcast.133, bf16[2048,2048]{1,0:T(8,128)(2,1)} %param.12), kind=kOutput, calls=%fused_computation.16 | convolution fusion | flops 17196644352 | bytes 25174016 | tf_op jit(solution)/shard_map/bsd,de->bse/dot_general | solution.py:34
  71.7 10.8 %fusion.11 = f32[16,128,2048]{2,1,0:T(8,128)} fusion(bf16[16,128,2048]{2,1,0:T(8,128)(2,1)} %get-tuple-element.20, f32[2048]{0:T(1024)S(1)} %convert_element_type.121, f32[16,128]{1,0:T(8,128)S(1)} %add_rsqrt_fusion.1), kind=kLoop, calls=%fused_computation.17 | loop fusion | flops 12582912 | bytes 25182208 | tf_op jit(solution)/shard_map/mul | solution.py:30
  82.6 14.1 %copy.33 = f32[256,8,16,128]{3,2,1,0:T(8,128)} copy(f32[256,8,16,128]{3,1,2,0:T(8,128)} %bitcast.108) | data formatting | bytes 33554432
  96.7 45.6 %fusion.200 = (f32[16,128,16,64]{3,2,1,0:T(8,128)}, f32[16,128,16,64]{3,2,1,0:T(8,128)}, f32[16,128,16,64]{3,2,1,0:T(8,128)}, f32[16,128,16,64]{3,2,1,0:T(8,128)}) fusion(f32[16,128,16,128]{3,2,1,0:T(8,128)} %bitcast.105, f32[16,128,16,128]{3,2,1,0:T(8,128)} %bitcast.106), kind=kLoop, calls=%fused_computation.202 | loop fusion | bytes 67108864 | tf_op jit(solution)/shard_map/slice | solution.py:23
  146.0 52.6 %subtract_convert_fusion.1 = (bf16[16,128,16,64]{3,1,0,2:T(8,128)(2,1)}, bf16[16,128,16,64]{3,1,0,2:T(8,128)(2,1)}, bf16[16,128,16,64]{3,1,0,2:T(8,128)(2,1)}, bf16[16,128,16,64]{3,1,0,2:T(8,128)(2,1)}) fusion(f32[16,128,16,64]{3,2,1,0:T(8,128)} %get-tuple-element.10, f32[16,128,16,64]{3,2,1,0:T(8,128)} %get-tuple-element.9, ...), kind=kLoop, calls=%fused_computation.28 | loop fusion | flops 33554432 | bytes 51380224 | tf_op jit(solution)/shard_map/convert.2
  198.6 11.4 %pad_maximum_fusion = bf16[16,128,16,128]{3,1,0,2:T(8,128)(2,1)} fusion(bf16[16,128,16,64]{3,1,0,2:T(8,128)(2,1)} %get-tuple-element.6, bf16[16,128,16,64]{3,1,0,2:T(8,128)(2,1)} %get-tuple-element.5), kind=kLoop, calls=%fused_computation.42 | loop fusion | flops 16777216 | bytes 16777216 | tf_op jit(solution)/shard_map/concatenate | solution.py:25
  210.0 6.0 all-to-all-start.1
  216.0 10.9 %pad_maximum_fusion.1 = bf16[16,128,16,128]{3,1,0,2:T(8,128)(2,1)} fusion(bf16[16,128,16,64]{3,1,0,2:T(8,128)(2,1)} %get-tuple-element.13, bf16[16,128,16,64]{3,1,0,2:T(8,128)(2,1)} %get-tuple-element.14), kind=kLoop, calls=%fused_computation.43 | loop fusion | flops 16777216 | bytes 16777216 | tf_op jit(solution)/shard_map/concatenate | solution.py:25
  226.9 82.5 %all-to-all-done.1 = bf16[16,128,16,128]{3,1,0,2:T(8,128)(2,1)} async-done(((bf16[16,128,16,128]{3,1,0,2:T(8,128)(2,1)}), bf16[16,128,16,128]{3,1,0,2:T(8,128)(2,1)}, u32[]{:S(2)}, u32[]{:S(2)}) %all-to-all-start.1) | async-done | bytes 8388640 | tf_op jit(solution)/shard_map/all_to_all | solution.py:66
  309.4 6.1 all-to-all-start.2
  315.5 23.5 %convert_bitcast_fusion = bf16[16,16,16,8,128]{4,3,2,1,0:T(8,128)(2,1)} fusion(bf16[16,128,2048]{2,1,0:T(8,128)(2,1)} %param.9, bf16[2048,2048]{1,0:T(8,128)(2,1)} %param.13), kind=kOutput, calls=%fused_computation.58 | convolution fusion | flops 17184063488 | bytes 25165824 | tf_op jit(solution)/shard_map/bsd,de->bse/dot_general | solution.py:34
  339.0 9.0 %copy.44 = bf16[16,16,16,8,128]{4,3,1,0,2:T(8,128)(2,1)} copy(bf16[16,16,16,8,128]{4,3,2,1,0:T(8,128)(2,1)} %convert_bitcast_fusion) | data formatting | bytes 16777216 | tf_op jit(solution)/shard_map/reshape | solution.py:65
  348.1 61.0 %all-to-all-done.2 = bf16[16,128,16,128]{3,1,0,2:T(8,128)(2,1)} async-done(((bf16[16,128,16,128]{3,1,0,2:T(8,128)(2,1)}), bf16[16,128,16,128]{3,1,0,2:T(8,128)(2,1)}, u32[]{:S(2)}, u32[]{:S(2)}) %all-to-all-start.2) | async-done | bytes 8388640 | tf_op jit(solution)/shard_map/all_to_all | solution.py:67
  409.1 6.1 all-to-all-start
  416.1 10.5 %copy.19 = bf16[16,128,8,2,128]{4,1,2,3,0:T(8,128)(2,1)} copy(bf16[16,128,8,2,128]{4,1,0,3,2:T(8,128)(2,1)} %bitcast.5) | data formatting | bytes 16777216 | tf_op jit(solution)/shard_map/all_to_all | solution.py:66
  426.6 10.5 %copy.22 = bf16[16,128,8,2,128]{4,1,2,3,0:T(8,128)(2,1)} copy(bf16[16,128,8,2,128]{4,1,0,3,2:T(8,128)(2,1)} %bitcast.9) | data formatting | bytes 16777216 | tf_op jit(solution)/shard_map/all_to_all | solution.py:67
  443.3 4.7 fusion.83
  448.0 6.5 fusion.76
  454.4 5.8 fusion.68
  460.3 7.1 fusion.60
  467.4 7.9 fusion.42
  475.3 8.8 %fusion.34 = f32[16,2,128,896]{3,2,1,0:T(8,128)} fusion(bf16[16,1024,2,128]{3,1,2,0:T(8,128)(2,1)S(1)} %bitcast.104, bf16[16,1024,2,128]{3,1,2,0:T(8,128)(2,1)} %bitcast.118), kind=kOutput, calls=%fused_computation.64 | convolution fusion | flops 939524096 | bytes 23068672 | tf_op jit(solution)/shard_map/bqhd,bkhd->bhqk/dot_general | solution.py:51
  484.0 11.8 %fusion.213 = (f32[16,2,128]{2,1,0:T(2,128)S(1)}, f32[16,2,128,1024]{3,2,1,0:T(8,128)}) fusion(pred[128,1024]{1,0:T(8,128)(4,1)S(1)} %iota_compare_fusion, bf16[16,1024,2,128]{3,1,2,0:T(8,128)(2,1)} %bitcast.98, bf16[16,1024,2,128]{3,1,2,0:T(8,128)(2,1)} %bitcast.119), kind=kOutput, calls=%fused_computation.211 | convolution fusion | flops 1090520064 | bytes 26361856 | tf_op jit(solution)/shard_map/sub | solution.py:54
  495.9 12.8 %all-to-all-done = bf16[16,128,16,128]{3,1,0,2:T(8,128)(2,1)} async-done(((bf16[16,128,16,128]{3,1,0,2:T(8,128)(2,1)}), bf16[16,128,16,128]{3,1,0,2:T(8,128)(2,1)}, u32[]{:S(2)}, u32[]{:S(2)}) %all-to-all-start) | async-done | bytes 8388640 | tf_op jit(solution)/shard_map/all_to_all | solution.py:68
  508.6 10.5 %copy.16 = bf16[16,128,8,2,128]{4,1,2,3,0:T(8,128)(2,1)} copy(bf16[16,128,8,2,128]{4,1,0,3,2:T(8,128)(2,1)} %bitcast.1) | data formatting | bytes 16777216 | tf_op jit(solution)/shard_map/all_to_all | solution.py:68
  519.2 19.0 %fusion.212 = (f32[16,2,128]{2,1,0:T(2,128)S(1)}, f32[16,2,128,896]{3,2,1,0:T(8,128)}) fusion(f32[16,2,128,896]{3,2,1,0:T(8,128)} %fusion.34, pred[128,896]{1,0:T(8,128)(4,1)S(1)} %iota_compare_fusion.1), kind=kOutput, calls=%fused_computation.210 | output fusion | flops 22020992 | bytes 29491200 | tf_op jit(solution)/shard_map/sub | solution.py:54
  538.2 16.4 %fusion.211 = (f32[16,2,128]{2,1,0:T(2,128)S(1)}, f32[16,2,128,768]{3,2,1,0:T(8,128)}) fusion(f32[16,2,128,768]{3,2,1,0:T(8,128)} %fusion.42, pred[128,768]{1,0:T(8,128)(4,1)S(1)} %iota_compare_fusion.2), kind=kOutput, calls=%fused_computation.209 | output fusion | flops 18875136 | bytes 25280512 | tf_op jit(solution)/shard_map/sub | solution.py:54
  554.6 7.2 fusion.210
  561.8 12.6 %fusion.209 = (f32[16,2,128]{2,1,0:T(2,128)S(1)}, f32[16,2,128,512]{3,2,1,0:T(8,128)}) fusion(f32[16,2,128,512]{3,2,1,0:T(8,128)} %fusion.68, pred[128,512]{1,0:T(8,128)(4,1)S(1)} %iota_compare_fusion.4), kind=kOutput, calls=%fused_computation.207 | output fusion | flops 12583423 | bytes 16859136 | tf_op jit(solution)/shard_map/sub | solution.py:54
  574.4 9.7 %fusion.208 = (f32[16,2,128]{2,1,0:T(2,128)S(1)}, f32[16,2,128,384]{3,2,1,0:T(8,128)}) fusion(f32[16,2,128,384]{3,2,1,0:T(8,128)} %fusion.76, pred[128,384]{1,0:T(8,128)(4,1)S(1)} %iota_compare_fusion.5), kind=kOutput, calls=%fused_computation.206 | output fusion | flops 9437567 | bytes 12648448 | tf_op jit(solution)/shard_map/sub | solution.py:54
  587.8 3.8 fusion.135
  591.6 4.8 fusion.131
  596.4 5.9 fusion.125
  602.3 5.9 fusion.119
  608.2 6.6 fusion.147
  614.8 9.3 %fusion.113 = bf16[16,1024,2,128]{3,1,2,0:T(8,128)(2,1)} fusion(bf16[16,1024,2,128]{3,1,2,0:T(8,128)(2,1)} %fusion.147, bf16[16,1024,2,128]{3,1,2,0:T(8,128)(2,1)} %bitcast.125, f32[16,2,128,768]{3,2,1,0:T(8,128)} %get-tuple-element.30, f32[16,2,128]{2,1,0:T(2,128)S(1)} %get-tuple-element.29), kind=kOutput, calls=%fused_computation.132 | convolution fusion | flops 812122112 | bytes 19939328 | tf_op jit(solution)/shard_map/bhqk,bkhd->bqhd/dot_general | solution.py:55
  624.1 10.5 %fusion.141 = bf16[16,1024,2,128]{3,1,2,0:T(8,128)(2,1)} fusion(bf16[16,1024,2,128]{3,1,2,0:T(8,128)(2,1)} %fusion.113, bf16[16,1024,2,128]{3,1,2,0:T(8,128)(2,1)} %bitcast.126, f32[16,2,128,896]{3,2,1,0:T(8,128)} %get-tuple-element.32, f32[16,2,128]{2,1,0:T(2,128)S(1)} %get-tuple-element.31), kind=kOutput, calls=%fused_computation.144 | convolution fusion | flops 947388416 | bytes 23085056 | tf_op jit(solution)/shard_map/bhqk,bkhd->bqhd/dot_general | solution.py:55
  634.6 11.6 %fusion.137 = bf16[16,1024,2,128]{3,1,2,0:T(8,128)(2,1)} fusion(bf16[16,1024,2,128]{3,1,2,0:T(8,128)(2,1)} %fusion.141, bf16[16,1024,2,128]{3,1,2,0:T(8,128)(2,1)} %bitcast.127, f32[16,2,128,1024]{3,2,1,0:T(8,128)} %get-tuple-element.34, f32[16,2,128]{2,1,0:T(2,128)S(1)} %get-tuple-element.33), kind=kOutput, calls=%fused_computation.142 | convolution fusion | flops 1082654720 | bytes 26230784 | tf_op jit(solution)/shard_map/bhqk,bkhd->bqhd/dot_general | solution.py:55
  646.1 16.4 %copy.24 = bf16[16,1024,2,128]{3,2,0,1:T(2,128)(2,1)} copy(bf16[16,1024,2,128]{3,1,2,0:T(8,128)(2,1)} %fusion.137) | data formatting | bytes 16777216 | tf_op jit(solution)/shard_map/concatenate | solution.py:56
  662.5 6.4 all-to-all-start.3
  669.0 93.5 %all-to-all-done.3 = bf16[16,1024,2,128]{3,2,0,1:T(2,128)(2,1)} async-done(((bf16[16,1024,2,128]{3,2,0,1:T(2,128)(2,1)}), bf16[16,1024,2,128]{3,2,0,1:T(2,128)(2,1)}, u32[]{:S(2)}, u32[]{:S(2)}) %all-to-all-start.3) | async-done | bytes 8388640 | tf_op jit(solution)/shard_map/all_to_all | solution.py:70
  762.4 8.0 copy.45
  770.4 14.4 %reshape.97 = bf16[16,128,2048]{2,1,0:T(8,128)(2,1)} reshape(bf16[16,128,8,2,128]{4,3,2,1,0:T(2,128)(2,1)} %bitcast.110) | data formatting | bytes 16777216 | tf_op jit(solution)/shard_map/reshape | solution.py:70
  784.8 22.4 %fusion.12 = (f32[16,128]{1,0:T(8,128)S(1)}, bf16[16,128,2048]{2,1,0:T(8,128)(2,1)S(1)}) fusion(bf16[16,128,2048]{2,1,0:T(8,128)(2,1)} %reshape.97, bf16[2048,2048]{1,0:T(8,128)(2,1)} %param.14), kind=kOutput, calls=%fused_computation.18 | convolution fusion | flops 17196644352 | bytes 25174016 | tf_op jit(solution)/shard_map/bsd,de->bse/dot_general | solution.py:34
  807.2 9.3 %fusion.15 = bf16[16,128,2048]{2,1,0:T(8,128)(2,1)} fusion(bf16[16,128,2048]{2,1,0:T(8,128)(2,1)S(1)} %get-tuple-element.36, bf16[16,128,2048]{2,1,0:T(8,128)(2,1)} %param.9, f32[2048]{0:T(1024)S(1)} %convert_element_type.148, f32[16,128]{1,0:T(8,128)S(1)} %add_rsqrt_fusion), kind=kLoop, calls=%fused_computation.21 | loop fusion | flops 25165824 | bytes 25182208 | tf_op jit(solution)/shard_map/convert_element_type | solution.py:72
  (61 shorter events, 15.1 us)
Async XLA Ops:
  0.6 23.6 %copy-start.2 = (bf16[2048]{0:T(1024)(128)(2,1)S(1)}, bf16[2048]{0:T(1024)(128)(2,1)}, u32[]{:S(2)}) copy-start(bf16[2048]{0:T(1024)(128)(2,1)} %param.15) | copy-start | bytes 12292
  24.2 25.3 %slice-start.7 = ((s8[8388608]{0:T(1024)(128)(4,1)}), s8[4194304]{0:T(1024)(128)(4,1)S(1)}, s32[]{:S(2)}) async-start(s8[8388608]{0:T(1024)(128)(4,1)} %bitcast.132), calls=%async_computation.11 | async-start | bytes 8388608
  35.2 14.3 %slice-start.8 = ((s8[8388608]{0:T(1024)(128)(4,1)}), s8[4194304]{0:T(1024)(128)(4,1)S(1)}, s32[]{:S(2)}) async-start(s8[8388608]{0:T(1024)(128)(4,1)} %bitcast.132), calls=%async_computation.12 | async-start | bytes 8388608
  49.5 22.2 %copy-start.3 = (bf16[2048]{0:T(1024)(128)(2,1)S(1)}, bf16[2048]{0:T(1024)(128)(2,1)}, u32[]{:S(2)}) copy-start(bf16[2048]{0:T(1024)(128)(2,1)} %param.16) | copy-start | bytes 12292
  82.6 14.1 %copy-start.1 = (s32[16,128]{1,0:T(8,128)S(1)}, s32[16,128]{1,0:T(8,128)}, u32[]{:S(2)}) copy-start(s32[16,128]{1,0:T(8,128)} %param.10) | copy-start | bytes 24580
  96.7 45.6 %copy-start.5 = (f32[64]{0:T(128)S(1)}, f32[64]{0:T(128)}, u32[]{:S(2)}) copy-start(f32[64]{0:T(128)} %negate_power_fusion) | copy-start | bytes 772
  210.0 99.5 %all-to-all-start.1 = ((bf16[16,128,16,128]{3,1,0,2:T(8,128)(2,1)}), bf16[16,128,16,128]{3,1,0,2:T(8,128)(2,1)}, u32[]{:S(2)}, u32[]{:S(2)}) async-start(bf16[16,128,16,128]{3,1,0,2:T(8,128)(2,1)} %pad_maximum_fusion), calls=%async_computation.1 | async-start | bytes 16777216 | tf_op jit(solution)/shard_map/all_to_all | solution.py:66
  309.4 99.7 %all-to-all-start.2 = ((bf16[16,128,16,128]{3,1,0,2:T(8,128)(2,1)}), bf16[16,128,16,128]{3,1,0,2:T(8,128)(2,1)}, u32[]{:S(2)}, u32[]{:S(2)}) async-start(bf16[16,128,16,128]{3,1,0,2:T(8,128)(2,1)} %pad_maximum_fusion.1), calls=%async_computation.2 | async-start | bytes 16777216 | tf_op jit(solution)/shard_map/all_to_all | solution.py:67
  409.1 99.5 %all-to-all-start = ((bf16[16,128,16,128]{3,1,0,2:T(8,128)(2,1)}), bf16[16,128,16,128]{3,1,0,2:T(8,128)(2,1)}, u32[]{:S(2)}, u32[]{:S(2)}) async-start(bf16[16,128,16,128]{3,1,0,2:T(8,128)(2,1)} %bitcast.109), calls=%async_computation | async-start | bytes 16777216 | tf_op jit(solution)/shard_map/all_to_all | solution.py:68
  443.3 11.2 %slice-start = ((s8[8388608]{0:T(1024)(128)(4,1)}), s8[4194304]{0:T(1024)(128)(4,1)S(1)}, s32[]{:S(2)}) async-start(s8[8388608]{0:T(1024)(128)(4,1)} %bitcast.99), calls=%async_computation.4 | async-start | bytes 8388608
  448.0 6.5 slice-start.1
  519.2 35.4 %slice-start.2 = ((s8[10485760]{0:T(1024)(128)(4,1)}), s8[2097152]{0:T(1024)(128)(4,1)S(1)}, s32[]{:S(2)}) async-start(s8[10485760]{0:T(1024)(128)(4,1)} %bitcast.120), calls=%async_computation.6 | async-start | bytes 4194304
  519.2 35.4 %slice-start.3 = ((s8[10485760]{0:T(1024)(128)(4,1)}), s8[4194304]{0:T(1024)(128)(4,1)S(1)}, s32[]{:S(2)}) async-start(s8[10485760]{0:T(1024)(128)(4,1)} %bitcast.120), calls=%async_computation.7 | async-start | bytes 8388608
  538.2 16.4 %slice-start.4 = ((s8[10485760]{0:T(1024)(128)(4,1)}), s8[4194304]{0:T(1024)(128)(4,1)S(1)}, s32[]{:S(2)}) async-start(s8[10485760]{0:T(1024)(128)(4,1)} %bitcast.120), calls=%async_computation.8 | async-start | bytes 8388608
  574.4 9.7 %copy-start = (f32[16,2,128,256]{3,2,1,0:T(8,128)S(1)}, f32[16,2,128,256]{3,2,1,0:T(8,128)}, u32[]{:S(2)}) copy-start(f32[16,2,128,256]{3,2,1,0:T(8,128)} %fusion.83) | copy-start | bytes 12582916
  591.6 10.7 %slice-start.5 = ((s8[8388608]{0:T(1024)(128)(4,1)}), s8[4194304]{0:T(1024)(128)(4,1)S(1)}, s32[]{:S(2)}) async-start(s8[8388608]{0:T(1024)(128)(4,1)} %bitcast.128), calls=%async_computation.9 | async-start | bytes 8388608
  596.4 5.9 slice-start.6
  662.5 6.5 copy-start.4
  662.5 99.9 %all-to-all-start.3 = ((bf16[16,1024,2,128]{3,2,0,1:T(2,128)(2,1)}), bf16[16,1024,2,128]{3,2,0,1:T(2,128)(2,1)}, u32[]{:S(2)}, u32[]{:S(2)}) async-start(bf16[16,1024,2,128]{3,2,0,1:T(2,128)(2,1)} %copy.24), calls=%async_computation.3 | async-start | bytes 16777216 | tf_op jit(solution)/shard_map/all_to_all | solution.py:70
where the time goes:
time: 826 us; the launch traced here: 817 us
  waiting for transfers between devices  250 us (30%)
  matrix products  209 us (25%)
  other arithmetic  180 us (22%)
  local copies, waits for them, and re-layouts  153 us (19%)
  starting transfers between devices  24.6 us (3%)
    all_to_all x1, waiting for transfers between devices, local_block(): lax.all_to_all(o_heads, 'sp', 1, 2, tiled=True)  93.5 us
    dot_general x4, matrix products, project(): jnp.einsum('bsd,de->bse', x_tok, weight, preferred_element_type=jnp.float32)  91.7 us
    all_to_all x1, waiting for transfers between devices, local_block(): q_heads = lax.all_to_all(q_loc, 'sp', 2, 1, tiled=True)  82.5 us
    sub x6, other arithmetic, causal_attention(): probs = jax.nn.softmax(scores, axis=-1).astype(jnp.bfloat16)  68.6 us
    all_to_all x1, waiting for transfers between devices, local_block(): k_heads = lax.all_to_all(k_loc, 'sp', 2, 1, tiled=True)  61 us
    dot_general x8, matrix products, causal_attention(): jnp.einsum('bhqk,bkhd->bqhd', probs, v_heads[:, :key_end], preferred_elem...  58.3 us
    another operation x1, other arithmetic  52.6 us
    slice x1, local copies, waits for them, and re-layouts, apply_rope(): first = heads_f32[..., :half]  45.6 us
  transfers between devices with their start and end apart: 4, of which 4 were waited for; matrix products, arithmetic and copies ran while one was open for 15% of the time, Pallas kernels for 0%

commit v1 on v0

v1 whole, which is shorter than its diff:
```python
import functools
import math

import jax
import jax.numpy as jnp
import numpy as np
from jax import lax
from jax.experimental import pallas as pl
from jax.experimental.pallas import tpu as pltpu
from jax.sharding import PartitionSpec as P

HEAD_DIM = 128
ROPE_THETA = 500000.0
NORM_EPS = 1e-6
SCALE = HEAD_DIM ** -0.5
EXP2_SCALE = SCALE * math.log2(math.e)
CORES = 2
MESH = pl.DeviceIdType.MESH
VMEM_LIMIT = 67043328
COMM = True

PIO2 = (1.5703125, 4.837512969970703125e-4, 7.54978995489188216e-8)


def cos_sin_rows(angles, lane_low):
    quad = jnp.floor(angles * (2.0 / math.pi) + 0.5)
    r = angles - quad * PIO2[0]
    r = r - quad * PIO2[1]
    r = r - quad * PIO2[2]
    r2 = r * r
    sin_r = r + r * r2 * (-1.6666654611e-1 + r2 * (8.3321608736e-3 + r2 * -1.9515295891e-4))
    cos_r = 1.0 - 0.5 * r2 + r2 * r2 * (4.166664568298827e-2 + r2 * (-1.388731625493765e-3 + r2 * 2.443315711809948e-5))
    quad = jnp.where(lane_low, quad, quad + 3.0)
    quad = quad - 4.0 * jnp.floor(quad * 0.25)
    odd = jnp.logical_or(quad == 1.0, quad == 3.0)
    val = jnp.where(odd, sin_r, cos_r)
    neg = jnp.logical_or(quad == 1.0, quad == 2.0)
    return jnp.where(neg, -val, val)


def block_kernel(n, x_hbm, pos_hbm, freq_ref, gq_ref, gk_ref, ga_ref, wq_hbm, wk_hbm, wv_hbm, wo_hbm, y_hbm,
                 wq, wk, wv, wo, xb, q, k, v, a_buf, posb, cosb, sinb,
                 w_sem, p_send, p_recv, x_send, x_recv, y_send, y_recv):
    batch, t_loc, width = x_hbm.shape
    n_seq = batch // n
    chips = n // CORES
    rows_blk = CORES * t_loc
    heads = width // HEAD_DIM
    me = lax.axis_index("sp")
    chip = me // CORES
    core = lax.rem(me, CORES)

    def peer(hop, swap):
        other = core if swap == 0 else 1 - core
        return lax.rem(chip + hop, chips) * CORES + other

    peers = [(0, 1)] + [(h, w) for w in range(CORES) for h in (1, chips - 1)] + [(h, w) for h in range(2, chips - 1) for w in range(CORES)]

    w_copies = []
    for idx, (src, dst) in enumerate(((wq_hbm, wq), (wk_hbm, wk), (wv_hbm, wv), (wo_hbm, wo))):
        cp = pltpu.make_async_copy(src, dst, w_sem.at[idx])
        w_copies.append(cp)
    pos_own = pltpu.make_async_copy(pos_hbm, posb.at[me], p_recv.at[0])
    pos_own.start()
    own = [pltpu.make_async_copy(x_hbm.at[me * n_seq + s], xb.at[s, pl.ds(pl.multiple_of(me * t_loc, t_loc), t_loc)], x_recv.at[s, 0]) for s in range(n_seq)]
    for cp in own:
        cp.start()
    for cp in w_copies:
        cp.start()

    sends = []
    if COMM:
        barrier = pltpu.get_barrier_semaphore()
        for hop, swap in peers:
            pl.semaphore_signal(barrier, inc=1, device_id={"sp": peer(hop, swap)}, device_id_type=MESH)
        pl.semaphore_wait(barrier, n - 1)
        my_rows = pl.ds(pl.multiple_of(me * t_loc, t_loc), t_loc)
        for hop, swap in peers:
            tag = hop * CORES + swap
            cp = pltpu.make_async_remote_copy(src_ref=pos_hbm, dst_ref=posb.at[me], send_sem=p_send.at[tag], recv_sem=p_recv.at[tag],
                                              device_id={"sp": peer(hop, swap)}, device_id_type=MESH)
            cp.start()
            sends.append(cp)
        for s in range(n_seq):
            for hop, swap in peers:
                tag = hop * CORES + swap
                to = peer(hop, swap)
                cp = pltpu.make_async_remote_copy(src_ref=x_hbm.at[to * n_seq + s], dst_ref=xb.at[s, my_rows],
                                                  send_sem=x_send.at[s, tag], recv_sem=x_recv.at[s, tag],
                                                  device_id={"sp": to}, device_id_type=MESH)
                cp.start()
                sends.append(cp)

    pos_own.wait()
    if COMM:
        for tag in range(1, n):
            pltpu.make_async_copy(pos_hbm, posb.at[0], p_recv.at[tag]).wait()
    for cp in w_copies:
        cp.wait()

    lane = lax.broadcasted_iota(jnp.int32, (t_loc, HEAD_DIM), 1)
    row = lax.broadcasted_iota(jnp.int32, (t_loc, HEAD_DIM), 0)
    lane_low = lane < HEAD_DIM // 2
    eye = lane == row
    tri = lane <= row

    def tables(s):
        def one(j, _):
            pos_row = posb[j, pl.ds(me * n_seq + s, 1), :].astype(jnp.float32)
            pos_col = jnp.sum(jnp.where(eye, jnp.broadcast_to(pos_row, (t_loc, HEAD_DIM)), 0.0), axis=1, keepdims=True)
            both = cos_sin_rows(pos_col * freq_ref[...], lane_low)
            turned = pltpu.roll(both, HEAD_DIM // 2, 1)
            at = pl.ds(pl.multiple_of(j * t_loc, t_loc), t_loc)
            cosb[at, :] = jnp.where(lane_low, both, turned)
            sinb[at, :] = jnp.where(lane_low, -turned, both)
            return 0
        lax.fori_loop(0, n, one, 0)

    NT = 256
    RC = 32

    def matmul(lhs, w, put):
        def one(j, _):
            at = pl.ds(pl.multiple_of(j * NT, NT), NT)
            put(at, jnp.dot(lhs(), w[:, at], preferred_element_type=jnp.float32).astype(jnp.bfloat16))
            return 0
        lax.fori_loop(0, width // NT, one, 0)

    def sum_sq(load):
        total = None
        for h in range(heads):
            t = load(h)
            total = t * t if total is None else total + t * t
        return lax.rsqrt(jnp.sum(total, axis=1, keepdims=True) * (1.0 / width) + NORM_EPS)

    def norm_rope(buf, base, gain):
        def one(i, _):
            at = pl.ds(pl.multiple_of(base + i * RC, RC), RC)
            load = lambda h: buf[at, h * HEAD_DIM:(h + 1) * HEAD_DIM].astype(jnp.float32)
            rs = sum_sq(load)
            cos_t = cosb[at, :]
            sin_t = sinb[at, :]
            for h in range(heads):
                cols = slice(h * HEAD_DIM, (h + 1) * HEAD_DIM)
                t = load(h) * rs * gain[:, cols].astype(jnp.float32)
                buf[at, cols] = (t * cos_t + pltpu.roll(t, HEAD_DIM // 2, 1) * sin_t).astype(jnp.bfloat16)
            return 0
        lax.fori_loop(0, rows_blk // RC, one, 0)

    HU = 2

    def attend(blk):
        for half in range(CORES):
            r0 = blk * rows_blk + half * t_loc
            kv = r0 + t_loc

            def some_heads(i, _, r0=r0, kv=kv):
                for u in range(HU):
                    cols = pl.ds(pl.multiple_of((i * HU + u) * HEAD_DIM, HEAD_DIM), HEAD_DIM)
                    q_h = q[r0:r0 + t_loc, cols]
                    s = lax.dot_general(q_h, k[0:kv, cols], (((1,), (1,)), ((), ())), preferred_element_type=jnp.float32)
                    last = jnp.where(tri, s[:, r0:], -1e30)
                    s = last if r0 == 0 else jnp.concatenate([s[:, :r0], last], axis=1)
                    m = jnp.max(s, axis=1, keepdims=True)
                    p = jnp.exp2((s - m) * EXP2_SCALE)
                    p = (p * (1.0 / jnp.sum(p, axis=1, keepdims=True))).astype(jnp.bfloat16)
                    q[r0:r0 + t_loc, cols] = jnp.dot(p, v[0:kv, cols], preferred_element_type=jnp.float32).astype(jnp.bfloat16)
                return 0
            lax.fori_loop(0, heads // HU, some_heads, 0)

    def hop_of(b, order):
        hop = order[-1]
        for i in range(len(order) - 1):
            hop = jnp.where(b == i, order[i], hop)
        return hop

    near = [h for h in (1, chips - 1)] + list(range(2, chips - 1))

    def sequence(s, _):
        tables(s)

        def project(b, _):
            hop = hop_of(b, [0] + near)
            c = lax.rem(chip + hop, chips)
            tag = lax.rem(chips - hop, chips) * CORES
            base = pl.multiple_of(c * rows_blk, rows_blk)
            rows = pl.ds(base, rows_blk)

            @pl.when(hop == 0)
            def _():
                pltpu.make_async_copy(x_hbm.at[0], xb.at[s, pl.ds(0, t_loc)], x_recv.at[s, 0]).wait()
                if COMM:
                    pltpu.make_async_copy(x_hbm.at[0], xb.at[s, pl.ds(0, t_loc)], x_recv.at[s, 1]).wait()

            if COMM:
                @pl.when(hop != 0)
                def _():
                    for w in range(CORES):
                        pltpu.make_async_copy(x_hbm.at[0], xb.at[s, pl.ds(0, t_loc)], x_recv.at[s, tag + w]).wait()

            lhs = lambda: xb[s, rows, :]

            def putter(buf):
                def put(at, val):
                    buf[rows, at] = val
                return put
            matmul(lhs, wq, putter(q))
            norm_rope(q, base, gq_ref)
            matmul(lhs, wk, putter(k))
            norm_rope(k, base, gk_ref)
            matmul(lhs, wv, putter(v))
            return 0
        lax.fori_loop(0, chips, project, 0)

        def finish(b, _):
            hop = hop_of(b, near + [0])
            c = lax.rem(chip + hop, chips)
            base = pl.multiple_of(c * rows_blk, rows_blk)
            rows = pl.ds(base, rows_blk)
            for blk in range(chips):
                @pl.when(c == blk)
                def _():
                    attend(blk)

            def put(at, val):
                a_buf[:, at] = val
            matmul(lambda: q[rows, :], wo, put)

            def out_rows(i, _):
                at = pl.ds(pl.multiple_of(i * RC, RC), RC)
                xat = pl.ds(pl.multiple_of(base + i * RC, RC), RC)
                load = lambda h: a_buf[at, h * HEAD_DIM:(h + 1) * HEAD_DIM].astype(jnp.float32)
                rs = sum_sq(load)
                for h in range(heads):
                    cols = slice(h * HEAD_DIM, (h + 1) * HEAD_DIM)
                    res = xb[s, xat, cols].astype(jnp.float32)
                    xb[s, xat, cols] = (res + load(h) * rs * ga_ref[:, cols].astype(jnp.float32)).astype(jnp.bfloat16)
                return 0
            lax.fori_loop(0, rows_blk // RC, out_rows, 0)

            def send(w):
                to = c * CORES + (core if w == 0 else 1 - core)
                src = xb.at[s, pl.ds(pl.multiple_of(to * t_loc, t_loc), t_loc)]
                pltpu.make_async_remote_copy(src_ref=src, dst_ref=y_hbm.at[me * n_seq + s], send_sem=y_send.at[s, hop * CORES + w],
                                             recv_sem=y_recv.at[s, hop * CORES + w], device_id={"sp": to}, device_id_type=MESH).start()

            @pl.when(hop == 0)
            def _():
                src = xb.at[s, pl.ds(pl.multiple_of(me * t_loc, t_loc), t_loc)]
                pltpu.make_async_copy(src, y_hbm.at[me * n_seq + s], y_recv.at[s, 0]).start()
                if COMM:
                    send(1)

            if COMM:
                @pl.when(hop != 0)
                def _():
                    send(0)
                    send(1)
            return 0
        lax.fori_loop(0, chips, finish, 0)
        return 0

    lax.fori_loop(0, n_seq, sequence, 0)

    for s in range(n_seq):
        for tag in range(n if COMM else 1):
            pltpu.make_async_copy(xb.at[s, pl.ds(0, t_loc)], y_hbm.at[0], y_recv.at[s, tag]).wait()
    if COMM:
        for s in range(n_seq):
            for tag in range(1, n):
                pltpu.make_async_copy(xb.at[s, pl.ds(0, t_loc)], y_hbm.at[0], y_send.at[s, tag]).wait()
        for cp in sends:
            cp.wait_send()


def solution(mesh):
    n = mesh.shape["sp"]

    def local_block(x_loc, pos_loc, w_query, w_key, w_value, w_out, gain_q, gain_k, gain_out):
        batch, t_loc, width = x_loc.shape
        n_seq = batch // n
        inv_freq = 1.0 / (ROPE_THETA ** (np.arange(0, HEAD_DIM, 2, dtype=np.float32) / HEAD_DIM))
        freq = jnp.asarray(np.concatenate([inv_freq, inv_freq]).astype(np.float32)[None, :])
        hbm = pl.BlockSpec(memory_space=pl.ANY)
        vmem = pl.BlockSpec(memory_space=pltpu.VMEM)
        seq = n * t_loc
        bf16 = jnp.bfloat16
        return pl.pallas_call(
            functools.partial(block_kernel, n),
            out_shape=jax.ShapeDtypeStruct(x_loc.shape, bf16),
            in_specs=[hbm, hbm, vmem, vmem, vmem, vmem, hbm, hbm, hbm, hbm],
            out_specs=hbm,
            scratch_shapes=[
                pltpu.VMEM((width, width), bf16), pltpu.VMEM((width, width), bf16), pltpu.VMEM((width, width), bf16), pltpu.VMEM((width, width), bf16),
                pltpu.VMEM((n_seq, seq, width), bf16),
                pltpu.VMEM((seq, width), bf16), pltpu.VMEM((seq, width), bf16), pltpu.VMEM((seq, width), bf16),
                pltpu.VMEM((CORES * t_loc, width), bf16),
                pltpu.VMEM((n, batch, t_loc), jnp.int32),
                pltpu.VMEM((seq, HEAD_DIM), jnp.float32), pltpu.VMEM((seq, HEAD_DIM), jnp.float32),
                pltpu.SemaphoreType.DMA((4,)),
                pltpu.SemaphoreType.DMA((n,)), pltpu.SemaphoreType.DMA((n,)),
                pltpu.SemaphoreType.DMA((n_seq, n)), pltpu.SemaphoreType.DMA((n_seq, n)),
                pltpu.SemaphoreType.DMA((n_seq, n)), pltpu.SemaphoreType.DMA((n_seq, n)),
            ],
            compiler_params=pltpu.CompilerParams(**({"collective_id": 0} if COMM else {}), has_side_effects=True, vmem_limit_bytes=VMEM_LIMIT),
            name="attention_block",
        )(x_loc, pos_loc, freq, gain_q[None, :], gain_k[None, :], gain_out[None, :], w_query, w_key, w_value, w_out)

    tok_spec = P("dp", "sp", None)
    return jax.shard_map(local_block, mesh=mesh, in_specs=(tok_spec, P("dp", "sp"), P(), P(), P(), P(), P(), P(), P()), out_specs=tok_spec, check_vma=False)
```

time: 826 us -> 348 us (0.42)
  the two profiles are of different devices: /device:TPU:113 before, /device:TPU:127 now
where the time goes in v1:
time: 348 us
  Pallas kernels  336 us (97%)
  local copies, waits for them, and re-layouts  12.3 us (4%)
    pallas_call x1, Pallas kernels, local_block(): pl.pallas_call(functools.partial(block_kernel, n), out_shape=jax.ShapeDty...  336 us
    unnamed x1, local copies, waits for them, and re-layouts  8.44 us

profile of v1, /device:TPU:127, one launch (start us, length us, event | category | flops | bytes accessed | tf_op | source)
XLA Modules:
  0.0 348.0 jit_solution(16409784073437943277)
XLA Ops:
  0.0 1.3 broadcast_in_dim.9.gq_ref
  1.3 1.3 broadcast_in_dim.10.gk_ref
  2.6 1.3 broadcast_in_dim.11.ga_ref
  3.9 335.7 %attention_block.1 = bf16[16,128,2048]{2,1,0:T(8,128)(2,1)} custom-call(bf16[16,128,2048]{2,1,0:T(8,128)(2,1)} %x_hbm.1, s32[16,128]{1,0:T(8,128)} %pos_hbm.1, f32[1,128]{1,0:T(1,128)} %constant.2.clone.freq_ref, bf16[1,2048]{1,0:T(2,128)(2,1)} %broadcast_in_dim.9.gq_ref, bf16[1,2048]{1,0:T(2,128)(2,1)} %broadcast_in_dim.10.gk_ref, ...), custom_call_target="tpu_custom_call" | custom-call | tf_op jit(solution)/shard_map/attention_block/pallas_call | solution.py:288
  339.6 8.4 %copy.12 = bf16[16,128,2048]{2,1,0:T(8,128)(2,1)} copy(bf16[16,128,2048]{2,1,0:T(8,128)(2,1)} %attention_block.1) | data formatting | bytes 16777216

commit v2 on v1

v2 whole, which is shorter than its diff:
```python
import functools
import math

import jax
import jax.numpy as jnp
import numpy as np
from jax import lax
from jax.experimental import pallas as pl
from jax.experimental.pallas import tpu as pltpu
from jax.sharding import PartitionSpec as P

HEAD_DIM = 128
ROPE_THETA = 500000.0
NORM_EPS = 1e-6
SCALE = HEAD_DIM ** -0.5
EXP2_SCALE = SCALE * math.log2(math.e)
CORES = 2
MESH = pl.DeviceIdType.MESH
VMEM_LIMIT = 67043328
NT = 1024
RG = 32

PIO2 = (1.5703125, 4.837512969970703125e-4, 7.54978995489188216e-8)


def cos_sin_rows(angles, lane_low):
    quad = jnp.floor(angles * (2.0 / math.pi) + 0.5)
    r = angles - quad * PIO2[0]
    r = r - quad * PIO2[1]
    r = r - quad * PIO2[2]
    r2 = r * r
    sin_r = r + r * r2 * (-1.6666654611e-1 + r2 * (8.3321608736e-3 + r2 * -1.9515295891e-4))
    cos_r = 1.0 - 0.5 * r2 + r2 * r2 * (4.166664568298827e-2 + r2 * (-1.388731625493765e-3 + r2 * 2.443315711809948e-5))
    quad = jnp.where(lane_low, quad, quad + 3.0)
    quad = quad - 4.0 * jnp.floor(quad * 0.25)
    odd = jnp.logical_or(quad == 1.0, quad == 3.0)
    val = jnp.where(odd, sin_r, cos_r)
    neg = jnp.logical_or(quad == 1.0, quad == 2.0)
    return jnp.where(neg, -val, val)


def block_kernel(n, x_hbm, pos_hbm, freq_ref, gains_ref, wq_hbm, wk_hbm, wv_hbm, wo_hbm, y_hbm,
                 wq, wk, wv, wo, xb, q, k, v, a_buf, s_buf, p_buf, posb, cosb, sinb,
                 w_sem, p_send, p_recv, x_send, x_recv, y_send, y_recv):
    batch, t_loc, width = x_hbm.shape
    n_seq = batch // n
    chips = n // CORES
    rows_blk = CORES * t_loc
    heads = width // HEAD_DIM
    me = lax.axis_index("sp")
    chip = me // CORES
    core = lax.rem(me, CORES)

    def peer(hop, swap):
        other = core if swap == 0 else 1 - core
        return lax.rem(chip + hop, chips) * CORES + other

    peers = [(0, 1)] + [(h, w) for w in range(CORES) for h in (1, chips - 1)] + [(h, w) for h in range(2, chips - 1) for w in range(CORES)]

    w_copies = []
    for idx, (src, dst) in enumerate(((wq_hbm, wq), (wk_hbm, wk), (wv_hbm, wv), (wo_hbm, wo))):
        cp = pltpu.make_async_copy(src, dst, w_sem.at[idx])
        w_copies.append(cp)
    pos_own = pltpu.make_async_copy(pos_hbm, posb.at[me], p_recv.at[0])
    pos_own.start()
    own = [pltpu.make_async_copy(x_hbm.at[me * n_seq + s], xb.at[s, pl.ds(pl.multiple_of(me * t_loc, t_loc), t_loc)], x_recv.at[s, 0]) for s in range(n_seq)]
    for cp in own:
        cp.start()
    for cp in w_copies:
        cp.start()

    sends = []
    barrier = pltpu.get_barrier_semaphore()
    for hop, swap in peers:
        pl.semaphore_signal(barrier, inc=1, device_id={"sp": peer(hop, swap)}, device_id_type=MESH)
    pl.semaphore_wait(barrier, n - 1)
    my_rows = pl.ds(pl.multiple_of(me * t_loc, t_loc), t_loc)
    for hop, swap in peers:
        tag = hop * CORES + swap
        cp = pltpu.make_async_remote_copy(src_ref=pos_hbm, dst_ref=posb.at[me], send_sem=p_send.at[tag], recv_sem=p_recv.at[tag],
                                          device_id={"sp": peer(hop, swap)}, device_id_type=MESH)
        cp.start()
        sends.append(cp)
    for s in range(n_seq):
        for hop, swap in peers:
            tag = hop * CORES + swap
            to = peer(hop, swap)
            cp = pltpu.make_async_remote_copy(src_ref=x_hbm.at[to * n_seq + s], dst_ref=xb.at[s, my_rows],
                                              send_sem=x_send.at[s, tag], recv_sem=x_recv.at[s, tag],
                                              device_id={"sp": to}, device_id_type=MESH)
            cp.start()
            sends.append(cp)

    pos_own.wait()
    for tag in range(1, n):
        pltpu.make_async_copy(pos_hbm, posb.at[0], p_recv.at[tag]).wait()

    lane = lax.broadcasted_iota(jnp.int32, (t_loc, HEAD_DIM), 1)
    row = lax.broadcasted_iota(jnp.int32, (t_loc, HEAD_DIM), 0)
    lane_low = lane < HEAD_DIM // 2
    eye = lane == row

    def tables(s):
        def one(j, _):
            pos_row = posb[j, pl.ds(me * n_seq + s, 1), :].astype(jnp.float32)
            pos_col = jnp.sum(jnp.where(eye, jnp.broadcast_to(pos_row, (t_loc, HEAD_DIM)), 0.0), axis=1, keepdims=True)
            both = cos_sin_rows(pos_col * freq_ref[...], lane_low)
            turned = pltpu.roll(both, HEAD_DIM // 2, 1)
            at = pl.ds(pl.multiple_of(j * t_loc, t_loc), t_loc)
            cosb[at, :] = jnp.where(lane_low, both, turned)
            sinb[at, :] = jnp.where(lane_low, -turned, both)
            return 0
        lax.fori_loop(0, n, one, 0)

    RC = 32
    n_iter = width // NT
    side_rows = rows_blk // n_iter

    def matmul(lhs, w, put, side=None):
        def one(j, _):
            at = pl.ds(pl.multiple_of(j * NT, NT), NT)
            put(at, jnp.dot(lhs(), w[:, at], preferred_element_type=jnp.float32).astype(jnp.bfloat16))
            if side is not None:
                for i in range(side_rows // RC):
                    side(j * (side_rows // RC) + i)
            return 0
        lax.fori_loop(0, n_iter, one, 0)

    def sum_sq(load):
        total = None
        for h in range(heads):
            t = load(h)
            total = t * t if total is None else total + t * t
        return lax.rsqrt(jnp.sum(total, axis=1, keepdims=True) * (1.0 / width) + NORM_EPS)

    def norm_rope(buf, base, gain):
        def one(i):
            at = pl.ds(pl.multiple_of(base + i * RC, RC), RC)
            load = lambda h: buf[at, h * HEAD_DIM:(h + 1) * HEAD_DIM].astype(jnp.float32)
            rs = sum_sq(load)
            cos_t = cosb[at, :]
            sin_t = sinb[at, :]
            for h in range(heads):
                cols = slice(h * HEAD_DIM, (h + 1) * HEAD_DIM)
                t = load(h) * rs * gains_ref[gain:gain + 1, cols].astype(jnp.float32)
                buf[at, cols] = (t * cos_t + pltpu.roll(t, HEAD_DIM // 2, 1) * sin_t).astype(jnp.bfloat16)
        return one

    def attend(blk):
        r0 = blk * rows_blk
        kv = r0 + rows_blk
        tri = lax.broadcasted_iota(jnp.int32, (RG, rows_blk), 1) - lax.broadcasted_iota(jnp.int32, (RG, rows_blk), 0)

        def cols_of(h):
            if isinstance(h, int):
                return slice(h * HEAD_DIM, (h + 1) * HEAD_DIM)
            return pl.ds(pl.multiple_of(h * HEAD_DIM, HEAD_DIM), HEAD_DIM)

        def scores(h, slot):
            cols = cols_of(h)
            s_buf[slot, :, 0:kv] = lax.dot_general(q[r0:kv, cols], k[0:kv, cols], (((1,), (1,)), ((), ())), preferred_element_type=jnp.float32)

        def soft(slot):
            for g in range(rows_blk // RG):
                s = s_buf[slot, g * RG:(g + 1) * RG, 0:kv]
                last = jnp.where(tri <= g * RG, s[:, r0:], -1e30)
                s = last if r0 == 0 else jnp.concatenate([s[:, :r0], last], axis=1)
                m = jnp.max(s, axis=1, keepdims=True)
                p = jnp.exp2((s - m) * EXP2_SCALE)
                p_buf[slot, g * RG:(g + 1) * RG, 0:kv] = (p * (1.0 / jnp.sum(p, axis=1, keepdims=True))).astype(jnp.bfloat16)

        def mix(h, slot):
            cols = cols_of(h)
            q[r0:kv, cols] = jnp.dot(p_buf[slot, :, 0:kv], v[0:kv, cols], preferred_element_type=jnp.float32).astype(jnp.bfloat16)

        scores(0, 0)
        scores(1, 1)
        soft(0)

        def pair(i, _):
            for u in range(2):
                h = 2 + 2 * i + u
                scores(h, u)
                soft(1 - u)
                mix(h - 2, u)
            return 0
        lax.fori_loop(0, heads // 2 - 1, pair, 0)
        soft(1)
        mix(heads - 2, 0)
        mix(heads - 1, 1)

    def hop_of(b, order):
        hop = order[-1]
        for i in range(len(order) - 1):
            hop = jnp.where(b == i, order[i], hop)
        return hop

    near = [h for h in (1, chips - 1)] + list(range(2, chips - 1))
    far = near[2:] + near[:2]

    def sequence(s, _):
        tables(s)

        def project(b, _):
            hop = hop_of(b, [0] + near)
            c = lax.rem(chip + hop, chips)
            tag = lax.rem(chips - hop, chips) * CORES
            base = pl.multiple_of(c * rows_blk, rows_blk)
            rows = pl.ds(base, rows_blk)

            @pl.when(hop == 0)
            def _():
                pltpu.make_async_copy(x_hbm.at[0], xb.at[s, pl.ds(0, t_loc)], x_recv.at[s, 0]).wait()
                pltpu.make_async_copy(x_hbm.at[0], xb.at[s, pl.ds(0, t_loc)], x_recv.at[s, 1]).wait()

            @pl.when(hop != 0)
            def _():
                for w in range(CORES):
                    pltpu.make_async_copy(x_hbm.at[0], xb.at[s, pl.ds(0, t_loc)], x_recv.at[s, tag + w]).wait()

            lhs = lambda: xb[s, rows, :]

            def putter(buf):
                def put(at, val):
                    buf[rows, at] = val
                return put

            def once(idx):
                @pl.when(jnp.logical_and(s == 0, b == 0))
                def _():
                    w_copies[idx].wait()
            once(0)
            matmul(lhs, wq, putter(q))
            once(1)
            matmul(lhs, wk, putter(k), norm_rope(q, base, 0))
            once(2)
            matmul(lhs, wv, putter(v), norm_rope(k, base, 1))
            return 0
        lax.fori_loop(0, chips, project, 0)

        def finish(b, _):
            hop = hop_of(b, far + [0])
            c = lax.rem(chip + hop, chips)
            base = pl.multiple_of(c * rows_blk, rows_blk)
            rows = pl.ds(base, rows_blk)
            for blk in range(chips):
                @pl.when(c == blk)
                def _():
                    attend(blk)

            def put(at, val):
                a_buf[:, at] = val
            @pl.when(jnp.logical_and(s == 0, b == 0))
            def _():
                w_copies[3].wait()
            matmul(lambda: q[rows, :], wo, put)

            def out_rows(i, _):
                at = pl.ds(pl.multiple_of(i * RC, RC), RC)
                xat = pl.ds(pl.multiple_of(base + i * RC, RC), RC)
                load = lambda h: a_buf[at, h * HEAD_DIM:(h + 1) * HEAD_DIM].astype(jnp.float32)
                rs = sum_sq(load)
                for h in range(heads):
                    cols = slice(h * HEAD_DIM, (h + 1) * HEAD_DIM)
                    res = xb[s, xat, cols].astype(jnp.float32)
                    xb[s, xat, cols] = (res + load(h) * rs * gains_ref[2:3, cols].astype(jnp.float32)).astype(jnp.bfloat16)
                return 0
            lax.fori_loop(0, rows_blk // RC, out_rows, 0)

            def send(w):
                to = c * CORES + (core if w == 0 else 1 - core)
                src = xb.at[s, pl.ds(pl.multiple_of(to * t_loc, t_loc), t_loc)]
                pltpu.make_async_remote_copy(src_ref=src, dst_ref=y_hbm.at[me * n_seq + s], send_sem=y_send.at[s, hop * CORES + w],
                                             recv_sem=y_recv.at[s, hop * CORES + w], device_id={"sp": to}, device_id_type=MESH).start()

            @pl.when(hop == 0)
            def _():
                src = xb.at[s, pl.ds(pl.multiple_of(me * t_loc, t_loc), t_loc)]
                pltpu.make_async_copy(src, y_hbm.at[me * n_seq + s], y_recv.at[s, 0]).start()
                send(1)

            @pl.when(hop != 0)
            def _():
                send(0)
                send(1)
            return 0
        lax.fori_loop(0, chips, finish, 0)
        return 0

    lax.fori_loop(0, n_seq, sequence, 0)

    for s in range(n_seq):
        for tag in range(n):
            pltpu.make_async_copy(xb.at[s, pl.ds(0, t_loc)], y_hbm.at[0], y_recv.at[s, tag]).wait()
    for s in range(n_seq):
        for tag in range(1, n):
            pltpu.make_async_copy(xb.at[s, pl.ds(0, t_loc)], y_hbm.at[0], y_send.at[s, tag]).wait()
    for cp in sends:
        cp.wait_send()


def solution(mesh):
    n = mesh.shape["sp"]

    def local_block(x_loc, pos_loc, w_query, w_key, w_value, w_out, gain_q, gain_k, gain_out):
        batch, t_loc, width = x_loc.shape
        n_seq = batch // n
        inv_freq = 1.0 / (ROPE_THETA ** (np.arange(0, HEAD_DIM, 2, dtype=np.float32) / HEAD_DIM))
        freq = jnp.asarray(np.concatenate([inv_freq, inv_freq]).astype(np.float32)[None, :])
        hbm = pl.BlockSpec(memory_space=pl.ANY)
        vmem = pl.BlockSpec(memory_space=pltpu.VMEM)
        seq = n * t_loc
        bf16 = jnp.bfloat16
        return pl.pallas_call(
            functools.partial(block_kernel, n),
            out_shape=jax.ShapeDtypeStruct(x_loc.shape, bf16),
            in_specs=[hbm, hbm, vmem, vmem, hbm, hbm, hbm, hbm],
            out_specs=hbm,
            scratch_shapes=[
                pltpu.VMEM((width, width), bf16), pltpu.VMEM((width, width), bf16), pltpu.VMEM((width, width), bf16), pltpu.VMEM((width, width), bf16),
                pltpu.VMEM((n_seq, seq, width), bf16),
                pltpu.VMEM((seq, width), bf16), pltpu.VMEM((seq, width), bf16), pltpu.VMEM((seq, width), bf16),
                pltpu.VMEM((CORES * t_loc, width), bf16),
                pltpu.VMEM((2, CORES * t_loc, seq), jnp.float32), pltpu.VMEM((2, CORES * t_loc, seq), bf16),
                pltpu.VMEM((n, batch, t_loc), jnp.int32),
                pltpu.VMEM((seq, HEAD_DIM), jnp.float32), pltpu.VMEM((seq, HEAD_DIM), jnp.float32),
                pltpu.SemaphoreType.DMA((4,)),
                pltpu.SemaphoreType.DMA((n,)), pltpu.SemaphoreType.DMA((n,)),
                pltpu.SemaphoreType.DMA((n_seq, n)), pltpu.SemaphoreType.DMA((n_seq, n)),
                pltpu.SemaphoreType.DMA((n_seq, n)), pltpu.SemaphoreType.DMA((n_seq, n)),
            ],
            compiler_params=pltpu.CompilerParams(collective_id=0, has_side_effects=True, vmem_limit_bytes=VMEM_LIMIT),
            name="attention_block",
        )(x_loc, pos_loc, freq, jnp.stack([gain_q, gain_k, gain_out]), w_query, w_key, w_value, w_out)

    tok_spec = P("dp", "sp", None)
    return jax.shard_map(local_block, mesh=mesh, in_specs=(tok_spec, P("dp", "sp"), P(), P(), P(), P(), P(), P(), P()), out_specs=tok_spec, check_vma=False)
```

time: 348 us -> 207 us (0.59)
  the two profiles are of different devices: /device:TPU:127 before, /device:TPU:113 now
where the time goes in v2:
time: 207 us
  Pallas kernels  196 us (95%)
  local copies, waits for them, and re-layouts  10.5 us (5%)
    pallas_call x1, Pallas kernels, local_block(): pl.pallas_call(functools.partial(block_kernel, n), out_shape=jax.ShapeDty...  196 us
    unnamed x1, local copies, waits for them, and re-layouts  8.44 us

profile of v2, /device:TPU:113, one launch (start us, length us, event | category | flops | bytes accessed | tf_op | source)
XLA Modules:
  0.0 207.1 jit_solution(4203711321922224315)
XLA Ops:
  0.0 0.7 stack.12
  0.7 0.7 stack.13
  1.4 0.7 stack.14
  2.1 0.6 pad_maximum_fusion.gains_ref
  2.7 195.9 %attention_block.1 = bf16[16,128,2048]{2,1,0:T(8,128)(2,1)} custom-call(bf16[16,128,2048]{2,1,0:T(8,128)(2,1)} %x_hbm.1, s32[16,128]{1,0:T(8,128)} %pos_hbm.1, f32[1,128]{1,0:T(1,128)} %constant.2.clone.freq_ref, bf16[3,2048]{1,0:T(4,128)(2,1)} %pad_maximum_fusion.gains_ref, bf16[2048,2048]{1,0:T(8,128)(2,1)} %wq_hbm.1, bf16[2048,2048]{1,0:T(8,128)(2,1)} %wk_hbm.1, ...), custom_call_target="tpu_custom_call" | custom-call | tf_op jit(solution)/shard_map/attention_block/pallas_call | solution.py:314
  198.6 8.4 %copy.12 = bf16[16,128,2048]{2,1,0:T(8,128)(2,1)} copy(bf16[16,128,2048]{2,1,0:T(8,128)(2,1)} %attention_block.1) | data formatting | bytes 16777216

commit v3 on v2

--- a/solution.py
+++ b/solution.py
@@ -19,6 +19,8 @@
 VMEM_LIMIT = 67043328
 NT = 1024
 RG = 32
+POST_U = 4
+YRC = 8
 
 PIO2 = (1.5703125, 4.837512969970703125e-4, 7.54978995489188216e-8)
 
@@ -39,8 +41,8 @@
     return jnp.where(neg, -val, val)
 
 
-def block_kernel(n, x_hbm, pos_hbm, freq_ref, gains_ref, wq_hbm, wk_hbm, wv_hbm, wo_hbm, y_hbm,
-                 wq, wk, wv, wo, xb, q, k, v, a_buf, s_buf, p_buf, posb, cosb, sinb,
+def block_kernel(n, x_hbm, pos_hbm, freq_ref, gq_ref, gk_ref, ga_ref, wq_hbm, wk_hbm, wv_hbm, wo_hbm, y_hbm,
+                 wq, wk, wv, wo, xb, q, k, v, a_buf, s_buf, p_buf, gains_ref, posb, cosb, sinb,
                  w_sem, p_send, p_recv, x_send, x_recv, y_send, y_recv):
     batch, t_loc, width = x_hbm.shape
     n_seq = batch // n
@@ -91,6 +93,9 @@
             cp.start()
             sends.append(cp)
 
+    for idx, g_ref in enumerate((gq_ref, gk_ref, ga_ref)):
+        gains_ref[idx:idx + 1, :] = g_ref[...].astype(jnp.float32).reshape(1, width)
+
     pos_own.wait()
     for tag in range(1, n):
         pltpu.make_async_copy(pos_hbm, posb.at[0], p_recv.at[tag]).wait()
@@ -100,17 +105,14 @@
     lane_low = lane < HEAD_DIM // 2
     eye = lane == row
 
-    def tables(s):
-        def one(j, _):
-            pos_row = posb[j, pl.ds(me * n_seq + s, 1), :].astype(jnp.float32)
-            pos_col = jnp.sum(jnp.where(eye, jnp.broadcast_to(pos_row, (t_loc, HEAD_DIM)), 0.0), axis=1, keepdims=True)
-            both = cos_sin_rows(pos_col * freq_ref[...], lane_low)
-            turned = pltpu.roll(both, HEAD_DIM // 2, 1)
-            at = pl.ds(pl.multiple_of(j * t_loc, t_loc), t_loc)
-            cosb[at, :] = jnp.where(lane_low, both, turned)
-            sinb[at, :] = jnp.where(lane_low, -turned, both)
-            return 0
-        lax.fori_loop(0, n, one, 0)
+    def table_rows(s, j):
+        pos_row = posb[j, pl.ds(me * n_seq + s, 1), :].astype(jnp.float32)
+        pos_col = jnp.sum(jnp.where(eye, jnp.broadcast_to(pos_row, (t_loc, HEAD_DIM)), 0.0), axis=1, keepdims=True)
+        both = cos_sin_rows(pos_col * freq_ref[...], lane_low)
+        turned = pltpu.roll(both, HEAD_DIM // 2, 1)
+        at = pl.ds(pl.multiple_of(j * t_loc, t_loc), t_loc)
+        cosb[at, :] = jnp.where(lane_low, both, turned)
+        sinb[at, :] = jnp.where(lane_low, -turned, both)
 
     RC = 32
     n_iter = width // NT
@@ -121,8 +123,7 @@
             at = pl.ds(pl.multiple_of(j * NT, NT), NT)
             put(at, jnp.dot(lhs(), w[:, at], preferred_element_type=jnp.float32).astype(jnp.bfloat16))
             if side is not None:
-                for i in range(side_rows // RC):
-                    side(j * (side_rows // RC) + i)
+                side(j)
             return 0
         lax.fori_loop(0, n_iter, one, 0)
 
@@ -134,7 +135,7 @@
         return lax.rsqrt(jnp.sum(total, axis=1, keepdims=True) * (1.0 / width) + NORM_EPS)
 
     def norm_rope(buf, base, gain):
-        def one(i):
+        def chunk(i):
             at = pl.ds(pl.multiple_of(base + i * RC, RC), RC)
             load = lambda h: buf[at, h * HEAD_DIM:(h + 1) * HEAD_DIM].astype(jnp.float32)
             rs = sum_sq(load)
@@ -142,8 +143,12 @@
             sin_t = sinb[at, :]
             for h in range(heads):
                 cols = slice(h * HEAD_DIM, (h + 1) * HEAD_DIM)
-                t = load(h) * rs * gains_ref[gain:gain + 1, cols].astype(jnp.float32)
+                t = load(h) * rs * gains_ref[gain:gain + 1, cols]
                 buf[at, cols] = (t * cos_t + pltpu.roll(t, HEAD_DIM // 2, 1) * sin_t).astype(jnp.bfloat16)
+
+        def one(j):
+            for i in range(side_rows // RC):
+                chunk(j * (side_rows // RC) + i)
         return one
 
     def attend(blk):
@@ -171,7 +176,10 @@
 
         def mix(h, slot):
             cols = cols_of(h)
-            q[r0:kv, cols] = jnp.dot(p_buf[slot, :, 0:kv], v[0:kv, cols], preferred_element_type=jnp.float32).astype(jnp.bfloat16)
+            first = h - slot
+            both = slice(first * HEAD_DIM, (first + 2) * HEAD_DIM) if isinstance(h, int) else pl.ds(pl.multiple_of(first * HEAD_DIM, 2 * HEAD_DIM), 2 * HEAD_DIM)
+            o = jnp.dot(p_buf[slot, :, 0:kv], v[0:kv, both], preferred_element_type=jnp.float32)
+            q[r0:kv, cols] = o[:, slot * HEAD_DIM:(slot + 1) * HEAD_DIM].astype(jnp.bfloat16)
 
         scores(0, 0)
         scores(1, 1)
@@ -199,7 +207,6 @@
     far = near[2:] + near[:2]
 
     def sequence(s, _):
-        tables(s)
 
         def project(b, _):
             hop = hop_of(b, [0] + near)
@@ -230,7 +237,7 @@
                 def _():
                     w_copies[idx].wait()
             once(0)
-            matmul(lhs, wq, putter(q))
+            matmul(lhs, wq, putter(q), (lambda j: table_rows(s, c * CORES + j)))
             once(1)
             matmul(lhs, wk, putter(k), norm_rope(q, base, 0))
             once(2)
@@ -255,7 +262,7 @@
                 w_copies[3].wait()
             matmul(lambda: q[rows, :], wo, put)
 
-            def out_rows(i, _):
+            def out_rows(i):
                 at = pl.ds(pl.multiple_of(i * RC, RC), RC)
                 xat = pl.ds(pl.multiple_of(base + i * RC, RC), RC)
                 load = lambda h: a_buf[at, h * HEAD_DIM:(h + 1) * HEAD_DIM].astype(jnp.float32)
@@ -263,9 +270,13 @@
                 for h in range(heads):
                     cols = slice(h * HEAD_DIM, (h + 1) * HEAD_DIM)
                     res = xb[s, xat, cols].astype(jnp.float32)
-                    xb[s, xat, cols] = (res + load(h) * rs * gains_ref[2:3, cols].astype(jnp.float32)).astype(jnp.bfloat16)
+                    xb[s, xat, cols] = (res + load(h) * rs * gains_ref[2:3, cols]).astype(jnp.bfloat16)
+
+            def out_group(i, _):
+                for u in range(POST_U):
+                    out_rows(i * POST_U + u)
                 return 0
-            lax.fori_loop(0, rows_blk // RC, out_rows, 0)
+            lax.fori_loop(0, rows_blk // RC // POST_U, out_group, 0)
 
             def send(w):
                 to = c * CORES + (core if w == 0 else 1 - core)
@@ -297,6 +308,19 @@
             pltpu.make_async_copy(xb.at[s, pl.ds(0, t_loc)], y_hbm.at[0], y_send.at[s, tag]).wait()
     for cp in sends:
         cp.wait_send()
+
+
+def copy_kernel(parts, src, dst, buf, in_sem, out_sem):
+    step = src.shape[0] // parts
+    reads = [pltpu.make_async_copy(src.at[pl.ds(i * step, step)], buf.at[pl.ds(i * step, step)], in_sem.at[i]) for i in range(parts)]
+    writes = [pltpu.make_async_copy(buf.at[pl.ds(i * step, step)], dst.at[pl.ds(i * step, step)], out_sem.at[i]) for i in range(parts)]
+    for cp in reads:
+        cp.start()
+    for i in range(parts):
+        reads[i].wait()
+        writes[i].start()
+    for cp in writes:
+        cp.wait()
 
 
 def solution(mesh):
@@ -311,10 +335,10 @@
         vmem = pl.BlockSpec(memory_space=pltpu.VMEM)
         seq = n * t_loc
         bf16 = jnp.bfloat16
-        return pl.pallas_call(
+        y_loc = pl.pallas_call(
             functools.partial(block_kernel, n),
             out_shape=jax.ShapeDtypeStruct(x_loc.shape, bf16),
-            in_specs=[hbm, hbm, vmem, vmem, hbm, hbm, hbm, hbm],
+            in_specs=[hbm, hbm, vmem, vmem, vmem, vmem, hbm, hbm, hbm, hbm],
             out_specs=hbm,
             scratch_shapes=[
                 pltpu.VMEM((width, width), bf16), pltpu.VMEM((width, width), bf16), pltpu.VMEM((width, width), bf16), pltpu.VMEM((width, width), bf16),
@@ -322,6 +346,7 @@
                 pltpu.VMEM((seq, width), bf16), pltpu.VMEM((seq, width), bf16), pltpu.VMEM((seq, width), bf16),
                 pltpu.VMEM((CORES * t_loc, width), bf16),
                 pltpu.VMEM((2, CORES * t_loc, seq), jnp.float32), pltpu.VMEM((2, CORES * t_loc, seq), bf16),
+                pltpu.VMEM((3, width), jnp.float32),
                 pltpu.VMEM((n, batch, t_loc), jnp.int32),
                 pltpu.VMEM((seq, HEAD_DIM), jnp.float32), pltpu.VMEM((seq, HEAD_DIM), jnp.float32),
                 pltpu.SemaphoreType.DMA((4,)),
@@ -331,7 +356,17 @@
             ],
             compiler_params=pltpu.CompilerParams(collective_id=0, has_side_effects=True, vmem_limit_bytes=VMEM_LIMIT),
             name="attention_block",
-        )(x_loc, pos_loc, freq, jnp.stack([gain_q, gain_k, gain_out]), w_query, w_key, w_value, w_out)
+        )(x_loc, pos_loc, freq, gain_q, gain_k, gain_out, w_query, w_key, w_value, w_out)
+        parts = YRC
+        return pl.pallas_call(
+            functools.partial(copy_kernel, parts),
+            out_shape=jax.ShapeDtypeStruct(x_loc.shape, bf16),
+            in_specs=[hbm],
+            out_specs=hbm,
+            scratch_shapes=[pltpu.VMEM(x_loc.shape, bf16), pltpu.SemaphoreType.DMA((parts,)), pltpu.SemaphoreType.DMA((parts,))],
+            compiler_params=pltpu.CompilerParams(vmem_limit_bytes=VMEM_LIMIT),
+            name="result_copy",
+        )(y_loc)
 
     tok_spec = P("dp", "sp", None)
     return jax.shard_map(local_block, mesh=mesh, in_specs=(tok_spec, P("dp", "sp"), P(), P(), P(), P(), P(), P(), P()), out_specs=tok_spec, check_vma=False)

time: 207 us -> 195 us (0.942)
  local copies, waits for them, and re-layouts: 10.5 us -> 0 us
    unnamed x1 -> x0, local copies, waits for them, and re-layouts: 8.44 us -> none
    pallas_call x1, Pallas kernels: 196 us -> 189 us  [local_block(): pl.pallas_call(functools.partial(block_kernel, n), out_shape=jax.ShapeDty...]
    pallas_call x0 -> x1, Pallas kernels: none -> 6.42 us  [local_block(): pl.pallas_call(functools.partial(copy_kernel, parts), out_shape=jax.Shape...]
    another operation x3 -> x0, local copies, waits for them, and re-layouts: 2.08 us -> none  [local_block(): jnp.stack([gain_q, gain_k, gain_out])]
where the time goes in v3:
time: 195 us
  Pallas kernels  195 us (100%)
    pallas_call x1, Pallas kernels, local_block(): pl.pallas_call(functools.partial(block_kernel, n), out_shape=jax.ShapeDty...  189 us
    pallas_call x1, Pallas kernels, local_block(): pl.pallas_call(functools.partial(copy_kernel, parts), out_shape=jax.Shape...  6.42 us

profile of v3, /device:TPU:113, one launch (start us, length us, event | category | flops | bytes accessed | tf_op | source)
XLA Modules:
  0.0 195.4 jit_solution(2113368172088036120)
XLA Ops:
  0.0 188.9 %attention_block.1.src = bf16[16,128,2048]{2,1,0:T(8,128)(2,1)} custom-call(bf16[16,128,2048]{2,1,0:T(8,128)(2,1)} %x_hbm.1, s32[16,128]{1,0:T(8,128)} %pos_hbm.1, f32[1,128]{1,0:T(1,128)} %constant.2.clone.freq_ref, bf16[2048]{0:T(1024)(128)(2,1)} %gq_ref.1, bf16[2048]{0:T(1024)(128)(2,1)} %gk_ref.1, bf16[2048]{0:T(1024)(128)(2,1)} %ga_ref.1, ...), custom_call_target="tpu_custom_call" | custom-call | tf_op jit(solution)/shard_map/attention_block/pallas_call | solution.py:338
  188.9 6.4 %result_copy.1 = bf16[16,128,2048]{2,1,0:T(8,128)(2,1)} custom-call(bf16[16,128,2048]{2,1,0:T(8,128)(2,1)} %attention_block.1.src), custom_call_target="tpu_custom_call" | custom-call | tf_op jit(solution)/shard_map/result_copy/pallas_call | solution.py:361

commit v4 on v3

--- a/solution.py
+++ b/solution.py
@@ -20,7 +20,6 @@
 NT = 1024
 RG = 32
 POST_U = 4
-YRC = 8
 
 PIO2 = (1.5703125, 4.837512969970703125e-4, 7.54978995489188216e-8)
 
@@ -41,14 +40,15 @@
     return jnp.where(neg, -val, val)
 
 
-def block_kernel(n, x_hbm, pos_hbm, freq_ref, gq_ref, gk_ref, ga_ref, wq_hbm, wk_hbm, wv_hbm, wo_hbm, y_hbm,
-                 wq, wk, wv, wo, xb, q, k, v, a_buf, s_buf, p_buf, gains_ref, posb, cosb, sinb,
-                 w_sem, p_send, p_recv, x_send, x_recv, y_send, y_recv):
+def block_kernel(n, x_hbm, pos_hbm, freq_hbm, gq_hbm, gk_hbm, ga_hbm, wq_hbm, wk_hbm, wv_hbm, wo_hbm, y_early, y_last,
+                 wq, wk, wv, wo, xb, q, k, v, a_buf, s_buf, p_buf, freq_ref, gq_ref, gk_ref, ga_ref, gains_ref, posb, cosb, sinb,
+                 w_sem, g_sem, p_send, p_recv, x_send, x_recv, y_send, y_recv):
     batch, t_loc, width = x_hbm.shape
     n_seq = batch // n
     chips = n // CORES
     rows_blk = CORES * t_loc
     heads = width // HEAD_DIM
+    y_outs = [y_early.at[s] for s in range(n_seq - 1)] + [y_last]
     me = lax.axis_index("sp")
     chip = me // CORES
     core = lax.rem(me, CORES)
@@ -58,6 +58,10 @@
         return lax.rem(chip + hop, chips) * CORES + other
 
     peers = [(0, 1)] + [(h, w) for w in range(CORES) for h in (1, chips - 1)] + [(h, w) for h in range(2, chips - 1) for w in range(CORES)]
+
+    barrier = pltpu.get_barrier_semaphore()
+    for hop, swap in peers:
+        pl.semaphore_signal(barrier, inc=1, device_id={"sp": peer(hop, swap)}, device_id_type=MESH)
 
     w_copies = []
     for idx, (src, dst) in enumerate(((wq_hbm, wq), (wk_hbm, wk), (wv_hbm, wv), (wo_hbm, wo))):
@@ -68,13 +72,15 @@
     own = [pltpu.make_async_copy(x_hbm.at[me * n_seq + s], xb.at[s, pl.ds(pl.multiple_of(me * t_loc, t_loc), t_loc)], x_recv.at[s, 0]) for s in range(n_seq)]
     for cp in own:
         cp.start()
+    small = []
+    for idx, (src, dst) in enumerate(((freq_hbm, freq_ref), (gq_hbm, gq_ref), (gk_hbm, gk_ref), (ga_hbm, ga_ref))):
+        cp = pltpu.make_async_copy(src, dst, g_sem.at[idx])
+        cp.start()
+        small.append(cp)
     for cp in w_copies:
         cp.start()
 
     sends = []
-    barrier = pltpu.get_barrier_semaphore()
-    for hop, swap in peers:
-        pl.semaphore_signal(barrier, inc=1, device_id={"sp": peer(hop, swap)}, device_id_type=MESH)
     pl.semaphore_wait(barrier, n - 1)
     my_rows = pl.ds(pl.multiple_of(me * t_loc, t_loc), t_loc)
     for hop, swap in peers:
@@ -93,6 +99,8 @@
             cp.start()
             sends.append(cp)
 
+    for cp in small:
+        cp.wait()
     for idx, g_ref in enumerate((gq_ref, gk_ref, ga_ref)):
         gains_ref[idx:idx + 1, :] = g_ref[...].astype(jnp.float32).reshape(1, width)
 
@@ -278,22 +286,23 @@
                 return 0
             lax.fori_loop(0, rows_blk // RC // POST_U, out_group, 0)
 
-            def send(w):
+            def send(w, dst):
                 to = c * CORES + (core if w == 0 else 1 - core)
                 src = xb.at[s, pl.ds(pl.multiple_of(to * t_loc, t_loc), t_loc)]
-                pltpu.make_async_remote_copy(src_ref=src, dst_ref=y_hbm.at[me * n_seq + s], send_sem=y_send.at[s, hop * CORES + w],
+                pltpu.make_async_remote_copy(src_ref=src, dst_ref=dst.at[me], send_sem=y_send.at[s, hop * CORES + w],
                                              recv_sem=y_recv.at[s, hop * CORES + w], device_id={"sp": to}, device_id_type=MESH).start()
 
-            @pl.when(hop == 0)
-            def _():
-                src = xb.at[s, pl.ds(pl.multiple_of(me * t_loc, t_loc), t_loc)]
-                pltpu.make_async_copy(src, y_hbm.at[me * n_seq + s], y_recv.at[s, 0]).start()
-                send(1)
-
-            @pl.when(hop != 0)
-            def _():
-                send(0)
-                send(1)
+            for s_now in range(n_seq):
+                @pl.when(jnp.logical_and(s == s_now, hop == 0))
+                def _():
+                    src = xb.at[s_now, pl.ds(pl.multiple_of(me * t_loc, t_loc), t_loc)]
+                    pltpu.make_async_copy(src, y_outs[s_now].at[me], y_recv.at[s_now, 0]).start()
+                    send(1, y_outs[s_now])
+
+                @pl.when(jnp.logical_and(s == s_now, hop != 0))
+                def _():
+                    send(0, y_outs[s_now])
+                    send(1, y_outs[s_now])
             return 0
         lax.fori_loop(0, chips, finish, 0)
         return 0
@@ -302,23 +311,23 @@
 
     for s in range(n_seq):
         for tag in range(n):
-            pltpu.make_async_copy(xb.at[s, pl.ds(0, t_loc)], y_hbm.at[0], y_recv.at[s, tag]).wait()
+            pltpu.make_async_copy(xb.at[s, pl.ds(0, t_loc)], y_outs[s].at[0], y_recv.at[s, tag]).wait()
     for s in range(n_seq):
         for tag in range(1, n):
-            pltpu.make_async_copy(xb.at[s, pl.ds(0, t_loc)], y_hbm.at[0], y_send.at[s, tag]).wait()
+            pltpu.make_async_copy(xb.at[s, pl.ds(0, t_loc)], y_outs[s].at[0], y_send.at[s, tag]).wait()
     for cp in sends:
         cp.wait_send()
 
 
-def copy_kernel(parts, src, dst, buf, in_sem, out_sem):
-    step = src.shape[0] // parts
-    reads = [pltpu.make_async_copy(src.at[pl.ds(i * step, step)], buf.at[pl.ds(i * step, step)], in_sem.at[i]) for i in range(parts)]
-    writes = [pltpu.make_async_copy(buf.at[pl.ds(i * step, step)], dst.at[pl.ds(i * step, step)], out_sem.at[i]) for i in range(parts)]
-    for cp in reads:
-        cp.start()
-    for i in range(parts):
-        reads[i].wait()
-        writes[i].start()
+def copy_kernel(early, last, dst, out_sem):
+    others, n = early.shape[:2]
+    writes = []
+    for i in range(n):
+        writes.append(pltpu.make_async_copy(last.at[i], dst.at[i * (others + 1) + others], out_sem.at[others, i]))
+        for s in range(others):
+            writes.append(pltpu.make_async_copy(early.at[s, i], dst.at[i * (others + 1) + s], out_sem.at[s, i]))
+    for cp in writes:
+        cp.start()
     for cp in writes:
         cp.wait()
 
@@ -332,41 +341,40 @@
         inv_freq = 1.0 / (ROPE_THETA ** (np.arange(0, HEAD_DIM, 2, dtype=np.float32) / HEAD_DIM))
         freq = jnp.asarray(np.concatenate([inv_freq, inv_freq]).astype(np.float32)[None, :])
         hbm = pl.BlockSpec(memory_space=pl.ANY)
-        vmem = pl.BlockSpec(memory_space=pltpu.VMEM)
         seq = n * t_loc
         bf16 = jnp.bfloat16
-        y_loc = pl.pallas_call(
+        early, last = pl.pallas_call(
             functools.partial(block_kernel, n),
-            out_shape=jax.ShapeDtypeStruct(x_loc.shape, bf16),
-            in_specs=[hbm, hbm, vmem, vmem, vmem, vmem, hbm, hbm, hbm, hbm],
-            out_specs=hbm,
+            out_shape=(pltpu.HBM((n_seq - 1, n, t_loc, width), bf16), pltpu.VMEM((n, t_loc, width), bf16)),
+            in_specs=[hbm] * 10,
+            out_specs=(hbm, hbm),
             scratch_shapes=[
                 pltpu.VMEM((width, width), bf16), pltpu.VMEM((width, width), bf16), pltpu.VMEM((width, width), bf16), pltpu.VMEM((width, width), bf16),
                 pltpu.VMEM((n_seq, seq, width), bf16),
                 pltpu.VMEM((seq, width), bf16), pltpu.VMEM((seq, width), bf16), pltpu.VMEM((seq, width), bf16),
                 pltpu.VMEM((CORES * t_loc, width), bf16),
                 pltpu.VMEM((2, CORES * t_loc, seq), jnp.float32), pltpu.VMEM((2, CORES * t_loc, seq), bf16),
+                pltpu.VMEM((1, HEAD_DIM), jnp.float32), pltpu.VMEM((width,), bf16), pltpu.VMEM((width,), bf16), pltpu.VMEM((width,), bf16),
                 pltpu.VMEM((3, width), jnp.float32),
                 pltpu.VMEM((n, batch, t_loc), jnp.int32),
                 pltpu.VMEM((seq, HEAD_DIM), jnp.float32), pltpu.VMEM((seq, HEAD_DIM), jnp.float32),
-                pltpu.SemaphoreType.DMA((4,)),
+                pltpu.SemaphoreType.DMA((4,)), pltpu.SemaphoreType.DMA((4,)),
                 pltpu.SemaphoreType.DMA((n,)), pltpu.SemaphoreType.DMA((n,)),
                 pltpu.SemaphoreType.DMA((n_seq, n)), pltpu.SemaphoreType.DMA((n_seq, n)),
                 pltpu.SemaphoreType.DMA((n_seq, n)), pltpu.SemaphoreType.DMA((n_seq, n)),
             ],
-            compiler_params=pltpu.CompilerParams(collective_id=0, has_side_effects=True, vmem_limit_bytes=VMEM_LIMIT),
+            compiler_params=pltpu.CompilerParams(collective_id=0, has_side_effects=True, vmem_limit_bytes=VMEM_LIMIT - seq * width * 2),
             name="attention_block",
         )(x_loc, pos_loc, freq, gain_q, gain_k, gain_out, w_query, w_key, w_value, w_out)
-        parts = YRC
         return pl.pallas_call(
-            functools.partial(copy_kernel, parts),
+            copy_kernel,
             out_shape=jax.ShapeDtypeStruct(x_loc.shape, bf16),
-            in_specs=[hbm],
+            in_specs=[pl.BlockSpec(memory_space=pltpu.VMEM), hbm],
             out_specs=hbm,
-            scratch_shapes=[pltpu.VMEM(x_loc.shape, bf16), pltpu.SemaphoreType.DMA((parts,)), pltpu.SemaphoreType.DMA((parts,))],
-            compiler_params=pltpu.CompilerParams(vmem_limit_bytes=VMEM_LIMIT),
+            scratch_shapes=[pltpu.SemaphoreType.DMA((n_seq, n))],
+            compiler_params=pltpu.CompilerParams(vmem_limit_bytes=VMEM_LIMIT // 4),
             name="result_copy",
-        )(y_loc)
+        )(early, last)
 
     tok_spec = P("dp", "sp", None)
     return jax.shard_map(local_block, mesh=mesh, in_specs=(tok_spec, P("dp", "sp"), P(), P(), P(), P(), P(), P(), P()), out_specs=tok_spec, check_vma=False)

time: 195 us -> 194 us (level)
  Pallas kernels: 195 us -> 192 us
  local copies, waits for them, and re-layouts: 0 us -> 2.18 us
    pallas_call x2, Pallas kernels: 195 us -> 192 us  [the longest x1 188 us: local_block(): pl.pallas_call(functools.partial(block_kernel, n), out_shape=(pltpu.HBM((...]
    unnamed x0 -> x2, local copies, waits for them, and re-layouts: none -> 2.18 us
where the time goes in v4:
time: 194 us
  Pallas kernels  192 us (99%)
  local copies, waits for them, and re-layouts  2.18 us (1%)
    pallas_call x1, Pallas kernels, local_block(): pl.pallas_call(functools.partial(block_kernel, n), out_shape=(pltpu.HBM((...  188 us

profile of v4, /device:TPU:113, one launch (start us, length us, event | category | flops | bytes accessed | tf_op | source)
XLA Modules:
  0.0 193.7 jit_solution(16656814123899993151)
XLA Ops:
  0.0 188.1 %attention_block.1 = (bf16[1,8,128,2048]{3,2,1,0:T(8,128)(2,1)}, bf16[8,128,2048]{2,1,0:T(8,128)(2,1)S(1)}) custom-call(bf16[16,128,2048]{2,1,0:T(8,128)(2,1)} %x_hbm.1, s32[16,128]{1,0:T(8,128)} %pos_hbm.1, f32[1,128]{1,0:T(1,128)} %constant.2.clone.freq_hbm, bf16[2048]{0:T(1024)(128)(2,1)} %gq_hbm.1, bf16[2048]{0:T(1024)(128)(2,1)} %gk_hbm.1, ...), custom_call_target="tpu_custom_call" | custom-call | tf_op jit(solution)/shard_map/attention_block/pallas_call | solution.py:346
  188.1 0.0 copy-start
  188.1 2.2 %copy-done = bf16[1,8,128,2048]{3,2,1,0:T(8,128)(2,1)S(1)} copy-done((bf16[1,8,128,2048]{3,2,1,0:T(8,128)(2,1)S(1)}, bf16[1,8,128,2048]{3,2,1,0:T(8,128)(2,1)}, u32[]{:S(2)}) %copy-start) | copy-done | bytes 4194328
  190.3 3.4 %result_copy.1 = bf16[16,128,2048]{2,1,0:T(8,128)(2,1)} custom-call(bf16[1,8,128,2048]{3,2,1,0:T(8,128)(2,1)S(1)} %copy-done, bf16[8,128,2048]{2,1,0:T(8,128)(2,1)S(1)} %get-tuple-element.8.last), custom_call_target="tpu_custom_call" | custom-call | tf_op jit(solution)/shard_map/result_copy/pallas_call | solution.py:369
Async XLA Ops:
  188.1 2.2 %copy-start = (bf16[1,8,128,2048]{3,2,1,0:T(8,128)(2,1)S(1)}, bf16[1,8,128,2048]{3,2,1,0:T(8,128)(2,1)}, u32[]{:S(2)}) copy-start(bf16[1,8,128,2048]{3,2,1,0:T(8,128)(2,1)} %get-tuple-element.7.early) | copy-start | bytes 12582916

commit v5 on v4

--- a/solution.py
+++ b/solution.py
@@ -19,7 +19,7 @@
 VMEM_LIMIT = 67043328
 NT = 1024
 RG = 32
-POST_U = 4
+POST_U = 8
 
 PIO2 = (1.5703125, 4.837512969970703125e-4, 7.54978995489188216e-8)
 

time: 194 us -> 194 us (level)
  no operation moved by 1% of the time
where the time goes in v5:
time: 194 us
  Pallas kernels  192 us (99%)
  local copies, waits for them, and re-layouts  2.18 us (1%)
    pallas_call x1, Pallas kernels, local_block(): pl.pallas_call(functools.partial(block_kernel, n), out_shape=(pltpu.HBM((...  188 us

profile of v5, /device:TPU:113, one launch (start us, length us, event | category | flops | bytes accessed | tf_op | source)
XLA Modules:
  0.0 193.7 jit_solution(18095360242970756609)
XLA Ops:
  0.0 188.1 %attention_block.1 = (bf16[1,8,128,2048]{3,2,1,0:T(8,128)(2,1)}, bf16[8,128,2048]{2,1,0:T(8,128)(2,1)S(1)}) custom-call(bf16[16,128,2048]{2,1,0:T(8,128)(2,1)} %x_hbm.1, s32[16,128]{1,0:T(8,128)} %pos_hbm.1, f32[1,128]{1,0:T(1,128)} %constant.2.clone.freq_hbm, bf16[2048]{0:T(1024)(128)(2,1)} %gq_hbm.1, bf16[2048]{0:T(1024)(128)(2,1)} %gk_hbm.1, ...), custom_call_target="tpu_custom_call" | custom-call | tf_op jit(solution)/shard_map/attention_block/pallas_call | solution.py:346
  188.1 0.0 copy-start
  188.1 2.2 %copy-done = bf16[1,8,128,2048]{3,2,1,0:T(8,128)(2,1)S(1)} copy-done((bf16[1,8,128,2048]{3,2,1,0:T(8,128)(2,1)S(1)}, bf16[1,8,128,2048]{3,2,1,0:T(8,128)(2,1)}, u32[]{:S(2)}) %copy-start) | copy-done | bytes 4194328
  190.3 3.4 %result_copy.1 = bf16[16,128,2048]{2,1,0:T(8,128)(2,1)} custom-call(bf16[1,8,128,2048]{3,2,1,0:T(8,128)(2,1)S(1)} %copy-done, bf16[8,128,2048]{2,1,0:T(8,128)(2,1)S(1)} %get-tuple-element.8.last), custom_call_target="tpu_custom_call" | custom-call | tf_op jit(solution)/shard_map/result_copy/pallas_call | solution.py:369
Async XLA Ops:
  188.1 2.2 %copy-start = (bf16[1,8,128,2048]{3,2,1,0:T(8,128)(2,1)S(1)}, bf16[1,8,128,2048]{3,2,1,0:T(8,128)(2,1)}, u32[]{:S(2)}) copy-start(bf16[1,8,128,2048]{3,2,1,0:T(8,128)(2,1)} %get-tuple-element.7.early) | copy-start | bytes 12582916
